TPU v7x, 32 devices: a whole 2x2x4 slice. The times are simulated.
32 devices in a mesh: member: 2 (over y), lat: 4 (over x, core), lon: 4 (over z).
Axes of the slice: x: 2, y: 2, z: 4, core: 2. Of those that a mesh axis runs over, the one named last changes fastest.
Arguments:
- field: bfloat16 [256, 512, 256], P(('member', 'lat'), 'lon'), parts along dimension 0, may hold values from -6 to 6
- mode_table: int32 [48], replicated, may hold values from 0 to 47, as said below
- analysis: bfloat16 [48, 48, 128], P(('lat', 'lon')), as said below
- synthesis: bfloat16 [48, 48, 128], P(('lat', 'lon')), as said below
- mixing: bfloat16 [1, 2, 256, 256], replicated, may hold values from -0.25 to 0.25
- degree_gain: float32 [1, 48, 256], replicated, may hold values from 0.25 to 1.75
- skip_weight: bfloat16 [1, 256, 256], replicated, may hold values from -0.375 to 0.375
Outputs:
- advanced: bfloat16 [256, 512, 256], P(('member', 'lat'), 'lon'), parts along dimension 0
- spectrum: bfloat16 [96, 48, 2, 256], P(('member', 'lat', 'lon')), parts along dimension 0
There are 2 independent parts, one for each index of `member`. A program takes and returns all parts, laid end to end along the dimension named above; an argument that names none is the same for every part. Nothing has to cross between parts.
Inputs may be any that keep to these rules, and one draw needn't show every extreme that they name: A permutation of 0 to 47; slot s of the spectral layout holds zonal wavenumber mode_table[s]. analysis[s, l, j] = weight[j] P(l, m, colat[j]) rounded to bfloat16, with m = mode_table[s], colat[j] = pi (j + 0.5) / 128, weight[j] = 2 pi^2 sin(colat[j]) / 65536, and P the orthonormal associated Legendre function of degree l and order m at cos(colat) without the Condon-Shortley phase, zero for l < m. synthesis[s, l, j] = c P(l, m, colat[j]) rounded to bfloat16, with m = mode_table[s], c = 1 where m = 0 and c = 2 elsewhere, P and colat as for analysis.
All inputs are finite; a program needn't handle non-finite values.
Results may differ from a plain program's by a relative error of at most 0.0062.
Values may be sent and summed in bfloat16 or wider, within the bound.
A program may use at most 64 MiB of HBM per device.

v0:
```python
import math
import jax
import jax.numpy as jnp
from jax import lax
from jax.sharding import PartitionSpec as P


def fourier_table(orders, length):
    phases = orders[:, None] * jnp.arange(length, dtype=jnp.int32)[None, :] % length
    angles = phases.astype(jnp.float32) * (2.0 * math.pi / length)
    return (
        jnp.stack([jnp.cos(angles), -jnp.sin(angles)], axis=1)
        .reshape(2 * orders.shape[0], length)
        .astype(jnp.bfloat16)
    )


def update(current, spectral, skip_matrix):
    shape_lead = current.shape
    direct = jnp.dot(
        current.reshape(-1, shape_lead[-1]), skip_matrix, preferred_element_type=jnp.float32
    ).reshape(shape_lead)
    pre_act = spectral.astype(jnp.float32) + direct
    return (current.astype(jnp.float32) + jax.nn.gelu(pre_act, approximate=False)).astype(
        jnp.bfloat16
    )


def per_device(field, mode_table, analysis, synthesis, mixing, degree_gain, skip_weight):
    lat_count = lax.axis_size("lat")
    lon_count = lax.axis_size("lon")
    lat_dev, lon_dev, channels = field.shape
    rows_full = lat_dev * lat_count
    points = lon_dev * lon_count
    mode_count = mode_table.shape[0]
    per_group = analysis.shape[0]
    forward = fourier_table(mode_table, points)
    mixed_last = None
    current = field
    row_block = lax.all_to_all(current, "lon", split_axis=0, concat_axis=1, tiled=True)
    lat_side = jnp.einsum(
        "rkc,qk->rqc", row_block, forward, preferred_element_type=jnp.float32
    ).astype(jnp.bfloat16)
    gathered = lax.all_to_all(lat_side, ("lat", "lon"), split_axis=1, concat_axis=0, tiled=True)
    lat_data = gathered.reshape(rows_full, per_group, 2 * channels)
    coefficients = jnp.einsum(
        "slj,jsx->slx", analysis, lat_data, preferred_element_type=jnp.float32
    ).astype(jnp.bfloat16)
    real_part = mixing[0, 0]
    imag_part = mixing[0, 1]
    joined = jnp.concatenate(
        [
            jnp.concatenate([real_part, imag_part], axis=1),
            jnp.concatenate([-imag_part, real_part], axis=1),
        ],
        axis=0,
    )
    product = jnp.dot(
        coefficients.reshape(-1, 2 * channels), joined, preferred_element_type=jnp.float32
    )
    product = product.reshape(per_group, mode_count, 2, channels)
    mixed_modes = (product * degree_gain[0][None, :, None, :]).astype(jnp.bfloat16)
    synthesized = jnp.einsum(
        "slj,slx->jsx",
        synthesis,
        mixed_modes.reshape(per_group, mode_count, 2 * channels),
        preferred_element_type=jnp.float32,
    )
    synthesized = synthesized.astype(jnp.bfloat16).reshape(rows_full, 2 * per_group, channels)
    returned = lax.all_to_all(synthesized, ("lat", "lon"), split_axis=0, concat_axis=1, tiled=True)
    spectral = jnp.einsum(
        "rqc,qk->rkc", returned, forward, preferred_element_type=jnp.float32
    ).astype(jnp.bfloat16)
    spectral, mixed_last = (spectral, mixed_modes)
    grid_part = lax.all_to_all(spectral, "lon", split_axis=1, concat_axis=0, tiled=True)
    current = update(current, grid_part, skip_weight[0])
    return (current, mixed_last)


def solution(mesh):
    in_specs = (
        P(("member", "lat"), "lon", None),
        P(),
        P(("lat", "lon"), None, None),
        P(("lat", "lon"), None, None),
        P(),
        P(),
        P(),
    )
    out_specs = (P(("member", "lat"), "lon", None), P(("member", "lat", "lon"), None, None, None))
    return jax.shard_map(
        per_device, mesh=mesh, in_specs=in_specs, out_specs=out_specs, check_vma=False
    )
```

profile of v0, /device:TPU:0, one launch (start us, length us, event | category | flops | bytes accessed | tf_op | source)
XLA Modules:
  0.0 162.0 jit_solution(3721329665403770944)
XLA Ops:
  0.6 0.0 copy-start
  0.6 0.0 copy-start.6
  0.7 6.5 %all-to-all-start = ((bf16[32,128,256]{2,1,0:T(8,128)(2,1)}), bf16[32,128,256]{2,1,0:T(8,128)(2,1)S(1)}, u32[]{:S(2)}, u32[]{:S(2)}) async-start(bf16[32,128,256]{2,1,0:T(8,128)(2,1)} %param.7), calls=%async_computation | async-start | bytes 4194304 | tf_op jit(solution)/shard_map/all_to_all | solution.py:40
  7.1 0.0 copy-done.6
  7.1 0.5 cosine_convert_fusion
  7.6 0.1 copy.50
  7.8 0.0 copy-start.2
  7.8 47.5 %all-to-all-done = bf16[32,128,256]{2,1,0:T(8,128)(2,1)S(1)} async-done(((bf16[32,128,256]{2,1,0:T(8,128)(2,1)}), bf16[32,128,256]{2,1,0:T(8,128)(2,1)S(1)}, u32[]{:S(2)}, u32[]{:S(2)}) %all-to-all-start) | async-done | bytes 2097184 | tf_op jit(solution)/shard_map/all_to_all | solution.py:40
  55.3 0.1 copy.51
  55.5 0.0 copy-start.3
  55.5 0.0 copy-start.4
  55.5 0.5 fusion.11
  56.0 0.0 copy-start.5
  56.0 1.0 copy.52
  57.0 3.8 %all-to-all-start.1 = ((bf16[8,96,256]{2,0,1:T(8,128)(2,1)}), bf16[8,96,256]{2,0,1:T(8,128)(2,1)S(1)}, u32[]{:S(2)}, u32[]{:S(2)}) async-start(bf16[8,96,256]{2,0,1:T(8,128)(2,1)} %copy.52), calls=%async_computation.1 | async-start | bytes 786432 | tf_op jit(solution)/shard_map/all_to_all | solution.py:44
  60.8 0.2 copy.55
  61.1 12.4 %all-to-all-done.1 = bf16[8,96,256]{2,0,1:T(8,128)(2,1)S(1)} async-done(((bf16[8,96,256]{2,0,1:T(8,128)(2,1)}), bf16[8,96,256]{2,0,1:T(8,128)(2,1)S(1)}, u32[]{:S(2)}, u32[]{:S(2)}) %all-to-all-start.1) | async-done | bytes 393248 | tf_op jit(solution)/shard_map/all_to_all | solution.py:44
  73.5 0.1 copy.53
  73.6 0.4 reshape.134
  74.0 0.4 fusion.12
  74.4 0.3 convolution_convert_fusion
  74.7 0.4 copy.57
  75.1 18.8 %all_to_all.60 = bf16[128,6,256]{2,1,0:T(8,128)(2,1)S(1)} all-to-all(bf16[128,6,256]{2,1,0:T(8,128)(2,1)S(1)} %copy.57), channel_id=1, replica_groups=mesh['member'=2,'lat'=4,'lon'=4] {'lat','lon'}, dimensions={0} | all-to-all | bytes 786432 | tf_op jit(solution)/shard_map/all_to_all | solution.py:70
  94.0 0.1 copy.59
  94.0 0.7 convert_bitcast_fusion
  94.8 2.5 %copy.61 = bf16[8,512,256]{2,0,1:T(8,128)(2,1)} copy(bf16[8,512,256]{2,1,0:T(8,128)(2,1)S(1)} %convert_bitcast_fusion) | data formatting | bytes 4194304 | tf_op jit(solution)/shard_map/convert_element_type | solution.py:73
  97.3 3.6 %all-to-all-start.3 = ((bf16[8,512,256]{2,0,1:T(8,128)(2,1)}), bf16[8,512,256]{2,0,1:T(8,128)(2,1)S(1)}, u32[]{:S(2)}, u32[]{:S(2)}) async-start(bf16[8,512,256]{2,0,1:T(8,128)(2,1)} %copy.61), calls=%async_computation.3 | async-start | bytes 4194304 | tf_op jit(solution)/shard_map/all_to_all | solution.py:75
  100.9 0.8 copy.56
  101.7 47.6 %all-to-all-done.3 = bf16[8,512,256]{2,0,1:T(8,128)(2,1)S(1)} async-done(((bf16[8,512,256]{2,0,1:T(8,128)(2,1)}), bf16[8,512,256]{2,0,1:T(8,128)(2,1)S(1)}, u32[]{:S(2)}, u32[]{:S(2)}) %all-to-all-start.3) | async-done | bytes 2097184 | tf_op jit(solution)/shard_map/all_to_all | solution.py:75
  149.3 0.6 copy.62
  149.9 1.0 copy-done.1
  150.9 11.1 %fusion.3 = bf16[32,128,256]{2,1,0:T(8,128)(2,1)} fusion(bf16[32,128,256]{2,1,0:T(8,128)(2,1)S(1)} %copy-done.1, f32[8,4,128,256]{3,2,0,1:T(8,128)S(1)} %copy.62, bf16[1,256,256]{2,1,0:T(8,128)(2,1)S(1)} %copy-done), kind=kOutput, calls=%fused_computation.4 | convolution fusion | flops 608174080 | bytes 8519680 | tf_op jit(solution)/shard_map/dot_general | solution.py:20
  (12 shorter events, 0.1 us)
Async XLA Ops:
  0.6 149.2 %copy-start = (bf16[1,256,256]{2,1,0:T(8,128)(2,1)S(1)}, bf16[1,256,256]{2,1,0:T(8,128)(2,1)}, u32[]{:S(2)}) copy-start(bf16[1,256,256]{2,1,0:T(8,128)(2,1)} %param.13) | copy-start | bytes 393220
  0.6 6.5 %copy-start.6 = (s32[48]{0:T(128)S(1)}, s32[48]{0:T(128)}, u32[]{:S(2)}) copy-start(s32[48]{0:T(128)} %param.8) | copy-start | bytes 580
  0.7 54.7 %all-to-all-start = ((bf16[32,128,256]{2,1,0:T(8,128)(2,1)}), bf16[32,128,256]{2,1,0:T(8,128)(2,1)S(1)}, u32[]{:S(2)}, u32[]{:S(2)}) async-start(bf16[32,128,256]{2,1,0:T(8,128)(2,1)} %param.7), calls=%async_computation | async-start | bytes 4194304 | tf_op jit(solution)/shard_map/all_to_all | solution.py:40
  7.8 52.9 %copy-start.2 = (bf16[1,2,256,256]{3,2,1,0:T(8,128)(2,1)S(1)}, bf16[1,2,256,256]{3,2,1,0:T(8,128)(2,1)}, u32[]{:S(2)}) copy-start(bf16[1,2,256,256]{3,2,1,0:T(8,128)(2,1)} %param.11) | copy-start | bytes 786436
  55.5 18.5 %copy-start.3 = (f32[1,48,256]{2,1,0:T(8,128)S(1)}, f32[1,48,256]{2,1,0:T(8,128)}, u32[]{:S(2)}) copy-start(f32[1,48,256]{2,1,0:T(8,128)} %param.12) | copy-start | bytes 147460
  55.5 18.5 %copy-start.4 = (bf16[3,48,128]{2,1,0:T(8,128)(2,1)S(1)}, bf16[3,48,128]{2,1,0:T(8,128)(2,1)}, u32[]{:S(2)}) copy-start(bf16[3,48,128]{2,1,0:T(8,128)(2,1)} %param.9) | copy-start | bytes 110596
  56.0 18.4 %copy-start.5 = (bf16[3,48,128]{2,1,0:T(8,128)(2,1)S(1)}, bf16[3,48,128]{2,1,0:T(8,128)(2,1)}, u32[]{:S(2)}) copy-start(bf16[3,48,128]{2,1,0:T(8,128)(2,1)} %param.10) | copy-start | bytes 110596
  57.0 16.5 %all-to-all-start.1 = ((bf16[8,96,256]{2,0,1:T(8,128)(2,1)}), bf16[8,96,256]{2,0,1:T(8,128)(2,1)S(1)}, u32[]{:S(2)}, u32[]{:S(2)}) async-start(bf16[8,96,256]{2,0,1:T(8,128)(2,1)} %copy.52), calls=%async_computation.1 | async-start | bytes 786432 | tf_op jit(solution)/shard_map/all_to_all | solution.py:44
  97.3 52.0 %all-to-all-start.3 = ((bf16[8,512,256]{2,0,1:T(8,128)(2,1)}), bf16[8,512,256]{2,0,1:T(8,128)(2,1)S(1)}, u32[]{:S(2)}, u32[]{:S(2)}) async-start(bf16[8,512,256]{2,0,1:T(8,128)(2,1)} %copy.61), calls=%async_computation.3 | async-start | bytes 4194304 | tf_op jit(solution)/shard_map/all_to_all | solution.py:75
  149.3 1.6 copy-start.1
where the time goes:
time: 162 us
  waiting for transfers between devices  108 us (67%)
  blocking collectives  18.8 us (12%)
  starting transfers between devices  13.9 us (9%)
  matrix products  13 us (8%)
  local copies, waits for them, and re-layouts  7.33 us (5%)
    all_to_all x1, waiting for transfers between devices, per_device(): lax.all_to_all(spectral, 'lon', split_axis=1, concat_axis=0, tiled=True)  47.6 us
    all_to_all x1, waiting for transfers between devices, per_device(): lax.all_to_all(current, 'lon', split_axis=0, concat_axis=1, tiled=True)  47.5 us
    all_to_all x1, blocking collectives, per_device(): lax.all_to_all(synthesized, ('lat', 'lon'), split_axis=0, concat_axis=1,...  18.8 us
    all_to_all x1, waiting for transfers between devices, per_device(): lax.all_to_all(lat_side, ('lat', 'lon'), split_axis=1, concat_axis=0, til...  12.4 us
    dot_general x1, matrix products, update(): jnp.dot(current.reshape(-1, shape_lead[-1]), skip_matrix, preferred_eleme...  11.1 us
    all_to_all x1, starting transfers between devices, per_device(): lax.all_to_all(current, 'lon', split_axis=0, concat_axis=1, tiled=True)  6.49 us
    all_to_all x1, starting transfers between devices, per_device(): lax.all_to_all(lat_side, ('lat', 'lon'), split_axis=1, concat_axis=0, til...  3.77 us
    all_to_all x1, starting transfers between devices, per_device(): lax.all_to_all(spectral, 'lon', split_axis=1, concat_axis=0, tiled=True)  3.61 us
  transfers between devices with their start and end apart: 3, of which 3 were waited for; matrix products, arithmetic and copies ran while one was open for 1% of the time, Pallas kernels for 0%

commit v1 on v0

--- a/solution.py
+++ b/solution.py
@@ -1,8 +1,43 @@
+import functools
 import math
 import jax
 import jax.numpy as jnp
 from jax import lax
 from jax.sharding import PartitionSpec as P
+
+
+def bring_space(mat, ndim_at, slab_in):
+    u_next = mat.shape
+    met_up = mat.reshape(
+        *u_next[:ndim_at], slab_in, u_next[ndim_at] // slab_in, *u_next[ndim_at + 1 :]
+    )
+    return jnp.moveaxis(met_up, ndim_at, 0)
+
+
+def slabs_divide(patch, d0):
+    b_next = list(patch.shape[1:])
+    b_next[d0] *= patch.shape[0]
+    return jnp.moveaxis(patch, 0, d0).reshape(b_next)
+
+
+def prepare_shards(x_part, peer_axis, panel, body):
+    before = lax.axis_size(peer_axis)
+    z1 = lax.axis_index(peer_axis)
+    z, w_next = (before, z1)
+    f_now = bring_space(x_part, panel, z)
+    mixed_arr = f_now
+    for q in range(1, z):
+        upper, earlier = ((w_next + q) % z, (w_next - q) % z)
+        passed = lax.dynamic_index_in_dim(f_now, upper, 0)
+        heard = range(z)
+        aux = map(lambda pp: (pp, (pp + q) % z), heard)
+        field_out = list(aux)
+        local_out = lax.ppermute(passed, peer_axis, field_out)
+        mixed_arr = lax.dynamic_update_slice_in_dim(mixed_arr, local_out, earlier, axis=0)
+    return slabs_divide(mixed_arr, body)
+
+
+stages_all_hold = functools.partial(prepare_shards, peer_axis="lon", panel=1, body=0)
 
 
 def fourier_table(orders, length):
@@ -72,7 +107,7 @@
         "rqc,qk->rkc", returned, forward, preferred_element_type=jnp.float32
     ).astype(jnp.bfloat16)
     spectral, mixed_last = (spectral, mixed_modes)
-    grid_part = lax.all_to_all(spectral, "lon", split_axis=1, concat_axis=0, tiled=True)
+    grid_part = stages_all_hold(spectral)
     current = update(current, grid_part, skip_weight[0])
     return (current, mixed_last)
 

time: 162 us -> 156 us (0.963)
  the two profiles are of different devices: /device:TPU:0 before, /device:TPU:8 now
where the time goes in v1:
time: 156 us; the launch traced here: 155 us
  waiting for transfers between devices  110 us (71%)
  starting transfers between devices  22.3 us (14%)
  matrix products  13 us (8%)
  local copies, waits for them, and re-layouts  8.7 us (6%)
    all_to_all x1, waiting for transfers between devices, per_device(): lax.all_to_all(current, 'lon', split_axis=0, concat_axis=1, tiled=True)  44.3 us
    ppermute x3, waiting for transfers between devices, prepare_shards(): local_out = lax.ppermute(passed, peer_axis, field_out)  41.6 us
    all_to_all x1, waiting for transfers between devices, per_device(): lax.all_to_all(synthesized, ('lat', 'lon'), split_axis=0, concat_axis=1,...  13.5 us
    dot_general x1, matrix products, update(): jnp.dot(current.reshape(-1, shape_lead[-1]), skip_matrix, preferred_eleme...  11.1 us
    all_to_all x1, waiting for transfers between devices, per_device(): lax.all_to_all(lat_side, ('lat', 'lon'), split_axis=1, concat_axis=0, til...  10.6 us
    all_to_all x1, starting transfers between devices, per_device(): lax.all_to_all(lat_side, ('lat', 'lon'), split_axis=1, concat_axis=0, til...  6.95 us
    all_to_all x1, starting transfers between devices, per_device(): lax.all_to_all(current, 'lon', split_axis=0, concat_axis=1, tiled=True)  5.46 us
    all_to_all x1, starting transfers between devices, per_device(): lax.all_to_all(synthesized, ('lat', 'lon'), split_axis=0, concat_axis=1,...  5.26 us
  transfers between devices with their start and end apart: 6, of which 6 were waited for; matrix products, arithmetic and copies ran while one was open for 2% of the time, Pallas kernels for 0%

profile of v1, /device:TPU:8, one launch (start us, length us, event | category | flops | bytes accessed | tf_op | source)
XLA Modules:
  0.0 155.4 jit_solution(1275662339331810975)
XLA Ops:
  0.6 0.0 copy-start
  0.7 5.5 %all-to-all-start = ((bf16[32,128,256]{2,1,0:T(8,128)(2,1)}), bf16[32,128,256]{2,1,0:T(8,128)(2,1)S(1)}, u32[]{:S(2)}, u32[]{:S(2)}) async-start(bf16[32,128,256]{2,1,0:T(8,128)(2,1)} %param.7), calls=%async_computation | async-start | bytes 4194304 | tf_op jit(solution)/shard_map/all_to_all | solution.py:75
  6.1 0.5 cosine_convert_fusion
  6.6 0.1 copy.48
  6.8 44.3 %all-to-all-done = bf16[32,128,256]{2,1,0:T(8,128)(2,1)S(1)} async-done(((bf16[32,128,256]{2,1,0:T(8,128)(2,1)}), bf16[32,128,256]{2,1,0:T(8,128)(2,1)S(1)}, u32[]{:S(2)}, u32[]{:S(2)}) %all-to-all-start) | async-done | bytes 2097184 | tf_op jit(solution)/shard_map/all_to_all | solution.py:75
  51.0 0.1 copy.49
  51.2 0.5 fusion.11
  51.7 1.0 copy.50
  52.7 7.0 %all-to-all-start.1 = ((bf16[8,96,256]{2,0,1:T(8,128)(2,1)}), bf16[8,96,256]{2,0,1:T(8,128)(2,1)S(1)}, u32[]{:S(2)}, u32[]{:S(2)}) async-start(bf16[8,96,256]{2,0,1:T(8,128)(2,1)} %copy.50), calls=%async_computation.1 | async-start | bytes 786432 | tf_op jit(solution)/shard_map/all_to_all | solution.py:79
  59.7 0.2 copy.53
  59.9 10.6 %all-to-all-done.1 = bf16[8,96,256]{2,0,1:T(8,128)(2,1)S(1)} async-done(((bf16[8,96,256]{2,0,1:T(8,128)(2,1)}), bf16[8,96,256]{2,0,1:T(8,128)(2,1)S(1)}, u32[]{:S(2)}, u32[]{:S(2)}) %all-to-all-start.1) | async-done | bytes 393248 | tf_op jit(solution)/shard_map/all_to_all | solution.py:79
  70.6 0.1 copy.51
  70.7 0.4 reshape.139
  71.1 0.4 fusion.12
  71.5 0.3 convolution_convert_fusion.1
  71.8 1.2 copy.55
  73.0 5.3 %all-to-all-start.2 = ((bf16[128,6,256]{2,1,0:T(8,128)(2,1)}), bf16[128,6,256]{2,1,0:T(8,128)(2,1)S(1)}, u32[]{:S(2)}, u32[]{:S(2)}) async-start(bf16[128,6,256]{2,1,0:T(8,128)(2,1)} %copy.55), calls=%async_computation.2 | async-start | bytes 1048576 | tf_op jit(solution)/shard_map/all_to_all | solution.py:105
  78.3 13.5 %all-to-all-done.2 = bf16[128,6,256]{2,1,0:T(8,128)(2,1)S(1)} async-done(((bf16[128,6,256]{2,1,0:T(8,128)(2,1)}), bf16[128,6,256]{2,1,0:T(8,128)(2,1)S(1)}, u32[]{:S(2)}, u32[]{:S(2)}) %all-to-all-start.2) | async-done | bytes 393248 | tf_op jit(solution)/shard_map/all_to_all | solution.py:105
  91.8 0.1 copy.57
  91.9 0.7 convolution_convert_fusion
  92.6 0.9 dynamic-slice_bitcast_fusion
  93.5 0.5 collective-permute-start
  94.1 4.0 %collective-permute-start.1 = (bf16[1,8,128,256]{3,2,0,1:T(8,128)(2,1)S(1)}, bf16[1,8,128,256]{3,2,0,1:T(8,128)(2,1)}, u32[]{:S(2)}, u32[]{:S(2)}) collective-permute-start(bf16[1,8,128,256]{3,2,0,1:T(8,128)(2,1)S(1)} %get-tuple-element.13), channel_id=1, source_target_pairs={{0,2},{1,3},{2,0},{3,1},{4,6},{5,7},{6,4},{7,5},{8,10},{9,11},{10,... | collective-permute-start | bytes 1572872 | tf_op jit(solution)/shard_map/ppermute | solution.py:35
  98.1 0.8 copy.54
  98.9 9.9 %collective-permute-done = bf16[1,8,128,256]{3,2,0,1:T(8,128)(2,1)} collective-permute-done((bf16[1,8,128,256]{3,2,0,1:T(8,128)(2,1)}, bf16[1,8,128,256]{3,2,0,1:T(8,128)(2,1)}, u32[]{:S(2)}, u32[]{:S(2)}) %collective-permute-start) | collective-permute-done | bytes 524320 | tf_op jit(solution)/shard_map/ppermute | solution.py:35
  108.9 1.1 constant_dynamic-update-slice_fusion.2
  109.9 29.9 %collective-permute-done.1 = bf16[1,8,128,256]{3,2,0,1:T(8,128)(2,1)} collective-permute-done((bf16[1,8,128,256]{3,2,0,1:T(8,128)(2,1)S(1)}, bf16[1,8,128,256]{3,2,0,1:T(8,128)(2,1)}, u32[]{:S(2)}, u32[]{:S(2)}) %collective-permute-start.1) | collective-permute-done | bytes 524320 | tf_op jit(solution)/shard_map/ppermute | solution.py:35
  139.9 1.1 constant_dynamic-update-slice_fusion.1
  141.0 1.7 %collective-permute-done.2 = bf16[1,8,128,256]{3,2,0,1:T(8,128)(2,1)} collective-permute-done((bf16[1,8,128,256]{3,2,0,1:T(8,128)(2,1)S(1)}, bf16[1,8,128,256]{3,2,0,1:T(8,128)(2,1)}, u32[]{:S(2)}, u32[]{:S(2)}) %collective-permute-start.2) | collective-permute-done | bytes 524320 | tf_op jit(solution)/shard_map/ppermute | solution.py:35
  142.7 1.1 constant_dynamic-update-slice_fusion
  143.8 0.5 copy.59
  144.3 11.1 %fusion.3 = bf16[32,128,256]{2,1,0:T(8,128)(2,1)} fusion(bf16[32,128,256]{2,1,0:T(8,128)(2,1)S(1)} %copy-done.1, f32[4,8,128,256]{3,2,1,0:T(8,128)S(1)} %copy.59, bf16[1,256,256]{2,1,0:T(8,128)(2,1)S(1)} %copy-done), kind=kOutput, calls=%fused_computation.4 | convolution fusion | flops 608174080 | bytes 8519680 | tf_op jit(solution)/shard_map/dot_general | solution.py:55
  (20 shorter events, 0.2 us)
Async XLA Ops:
  0.6 143.6 %copy-start = (bf16[1,256,256]{2,1,0:T(8,128)(2,1)S(1)}, bf16[1,256,256]{2,1,0:T(8,128)(2,1)}, u32[]{:S(2)}) copy-start(bf16[1,256,256]{2,1,0:T(8,128)(2,1)} %param.13) | copy-start | bytes 393220
  0.6 5.5 %copy-start.6 = (s32[48]{0:T(128)S(1)}, s32[48]{0:T(128)}, u32[]{:S(2)}) copy-start(s32[48]{0:T(128)} %param.8) | copy-start | bytes 580
  0.7 50.4 %all-to-all-start = ((bf16[32,128,256]{2,1,0:T(8,128)(2,1)}), bf16[32,128,256]{2,1,0:T(8,128)(2,1)S(1)}, u32[]{:S(2)}, u32[]{:S(2)}) async-start(bf16[32,128,256]{2,1,0:T(8,128)(2,1)} %param.7), calls=%async_computation | async-start | bytes 4194304 | tf_op jit(solution)/shard_map/all_to_all | solution.py:75
  6.8 52.8 %copy-start.2 = (bf16[1,2,256,256]{3,2,1,0:T(8,128)(2,1)S(1)}, bf16[1,2,256,256]{3,2,1,0:T(8,128)(2,1)}, u32[]{:S(2)}) copy-start(bf16[1,2,256,256]{3,2,1,0:T(8,128)(2,1)} %param.11) | copy-start | bytes 786436
  51.2 19.9 %copy-start.3 = (f32[1,48,256]{2,1,0:T(8,128)S(1)}, f32[1,48,256]{2,1,0:T(8,128)}, u32[]{:S(2)}) copy-start(f32[1,48,256]{2,1,0:T(8,128)} %param.12) | copy-start | bytes 147460
  51.2 19.9 %copy-start.4 = (bf16[3,48,128]{2,1,0:T(8,128)(2,1)S(1)}, bf16[3,48,128]{2,1,0:T(8,128)(2,1)}, u32[]{:S(2)}) copy-start(bf16[3,48,128]{2,1,0:T(8,128)(2,1)} %param.9) | copy-start | bytes 110596
  51.7 19.8 %copy-start.5 = (bf16[3,48,128]{2,1,0:T(8,128)(2,1)S(1)}, bf16[3,48,128]{2,1,0:T(8,128)(2,1)}, u32[]{:S(2)}) copy-start(bf16[3,48,128]{2,1,0:T(8,128)(2,1)} %param.10) | copy-start | bytes 110596
  52.7 17.9 %all-to-all-start.1 = ((bf16[8,96,256]{2,0,1:T(8,128)(2,1)}), bf16[8,96,256]{2,0,1:T(8,128)(2,1)S(1)}, u32[]{:S(2)}, u32[]{:S(2)}) async-start(bf16[8,96,256]{2,0,1:T(8,128)(2,1)} %copy.50), calls=%async_computation.1 | async-start | bytes 786432 | tf_op jit(solution)/shard_map/all_to_all | solution.py:79
  73.0 18.8 %all-to-all-start.2 = ((bf16[128,6,256]{2,1,0:T(8,128)(2,1)}), bf16[128,6,256]{2,1,0:T(8,128)(2,1)S(1)}, u32[]{:S(2)}, u32[]{:S(2)}) async-start(bf16[128,6,256]{2,1,0:T(8,128)(2,1)} %copy.55), calls=%async_computation.2 | async-start | bytes 1048576 | tf_op jit(solution)/shard_map/all_to_all | solution.py:105
  93.5 15.3 %collective-permute-start = (bf16[1,8,128,256]{3,2,0,1:T(8,128)(2,1)}, bf16[1,8,128,256]{3,2,0,1:T(8,128)(2,1)}, u32[]{:S(2)}, u32[]{:S(2)}) collective-permute-start(bf16[1,8,128,256]{3,2,0,1:T(8,128)(2,1)} %get-tuple-element.14), channel_id=1, source_target_pairs={{0,1},{1,2},{2,3},{3,0},{4,5},{5,6},{6,7},{7,4},{8,9},{9,10},{10,1... | collective-permute-start | bytes 1572872 | tf_op jit(solution)/shard_map/ppermute | solution.py:35
  94.1 45.8 %collective-permute-start.1 = (bf16[1,8,128,256]{3,2,0,1:T(8,128)(2,1)S(1)}, bf16[1,8,128,256]{3,2,0,1:T(8,128)(2,1)}, u32[]{:S(2)}, u32[]{:S(2)}) collective-permute-start(bf16[1,8,128,256]{3,2,0,1:T(8,128)(2,1)S(1)} %get-tuple-element.13), channel_id=1, source_target_pairs={{0,2},{1,3},{2,0},{3,1},{4,6},{5,7},{6,4},{7,5},{8,10},{9,11},{10,... | collective-permute-start | bytes 1572872 | tf_op jit(solution)/shard_map/ppermute | solution.py:35
  98.1 44.6 %collective-permute-start.2 = (bf16[1,8,128,256]{3,2,0,1:T(8,128)(2,1)S(1)}, bf16[1,8,128,256]{3,2,0,1:T(8,128)(2,1)}, u32[]{:S(2)}, u32[]{:S(2)}) collective-permute-start(bf16[1,8,128,256]{3,2,0,1:T(8,128)(2,1)S(1)} %get-tuple-element.12), channel_id=1, source_target_pairs={{0,3},{1,0},{2,1},{3,2},{4,7},{5,4},{6,5},{7,6},{8,11},{9,8},{10,9... | collective-permute-start | bytes 1572872 | tf_op jit(solution)/shard_map/ppermute | solution.py:35
  109.9 34.4 %copy-start.1 = (bf16[32,128,256]{2,1,0:T(8,128)(2,1)S(1)}, bf16[32,128,256]{2,1,0:T(8,128)(2,1)}, u32[]{:S(2)}) copy-start(bf16[32,128,256]{2,1,0:T(8,128)(2,1)} %param.7) | copy-start | bytes 6291460
